TPU v7x, 128 devices: a whole 4x4x4 slice. The times are simulated.
128 devices in a mesh: batch: 1, row: 16 (over z, y), col: 8 (over x, core).
Axes of the slice: x: 4, y: 4, z: 4, core: 2. Of those that a mesh axis runs over, the one named last changes fastest.
Arguments:
- lower_mat: bfloat16 [16384, 16384], P('row', 'col')
- rhs_mat: bfloat16 [16384, 2048], P('row', ('batch', 'col'))
Outputs:
- output: bfloat16 [16384, 2048], P('row', ('batch', 'col'))
All inputs are finite; a program needn't handle non-finite values.
Results may differ from a plain program's by a relative error of at most 0.001.
Values are sent between devices in bfloat16 or wider.
A program may use at most 1 GiB of HBM per device.

v0:
```python
import jax
import jax.numpy as jnp
from jax import lax
from jax.sharding import PartitionSpec as P

BLOCK_SIZE = 256


def solution(mesh):
    grid_rows = mesh.shape["row"]
    grid_cols = mesh.shape["col"]

    def local_product(lower_loc, rhs_loc):
        rows_loc = lower_loc.shape[0]
        rhs_cols = rhs_loc.shape[1]
        row_blocks = rows_loc // BLOCK_SIZE
        col_blocks = lower_loc.shape[1] // BLOCK_SIZE
        gathered_rhs = lax.all_gather(rhs_loc, "row", axis=0)
        rhs_steps = gathered_rhs.reshape(grid_rows, row_blocks, BLOCK_SIZE, rhs_cols).transpose(1, 0, 2, 3).reshape(col_blocks, grid_cols * BLOCK_SIZE, rhs_cols)
        block_sum = jnp.zeros((rows_loc, rhs_cols), jnp.float32)
        for step in range(col_blocks):
            first_row = (step * grid_cols // grid_rows) * BLOCK_SIZE
            panel = lower_loc[first_row:, step * BLOCK_SIZE:(step + 1) * BLOCK_SIZE]
            panels = lax.all_gather(panel, "col", axis=1, tiled=True)
            update = jnp.dot(panels, rhs_steps[step], preferred_element_type=jnp.float32)
            block_sum = lax.dynamic_update_slice(block_sum, block_sum[first_row:] + update, (first_row, 0))
        return block_sum.astype(jnp.bfloat16)

    return jax.shard_map(local_product, mesh=mesh, in_specs=(P("row", "col"), P("row", ("batch", "col"))), out_specs=P("row", ("batch", "col")), check_vma=False)
```

profile of v0, /device:TPU:0, one launch (start us, length us, event | category | flops | bytes accessed | tf_op | source)
XLA Modules:
  0.0 341.1 jit_solution(289710235059195700)
XLA Ops:
  6.5 0.7 all-gather.27.cloned.1.call-update
  7.3 2.3 fusion.5
  9.6 0.0 all-gather.13.cloned.1.call-start
  9.6 0.7 all-gather.13.cloned.1.call-update
  10.4 2.1 fusion.4
  12.5 0.5 all-gather.17.cloned.1.call-update
  13.1 1.9 fusion.3
  15.0 0.0 all-gather.21.cloned.1.call-start
  15.0 0.7 all-gather.21.cloned.1.call-update
  15.8 1.7 fusion.2
  17.5 0.0 all-gather.25.cloned.1.call-start
  17.6 0.7 all-gather.25.cloned.1.call-update
  18.3 64.5 %all-gather.27.cloned.1.call-done = bf16[16384,256]{1,0:T(8,128)(2,1)} async-done(((bf16[1024,256]{1,0:T(8,128)(2,1)}), bf16[16384,256]{1,0:T(8,128)(2,1)}) %all-gather.27.cloned.1.call-update) | async-done | bytes 8388624 | tf_op jit(solution)/shard_map/all_gather | solution.py:18
  82.8 7.6 %copy.3 = bf16[4,16,256,256]{3,2,1,0:T(8,128)(2,1)} copy(bf16[4,16,256,256]{3,2,0,1:T(8,128)(2,1)} %bitcast.52) | data formatting | bytes 16777216 | tf_op jit(solution)/shard_map/transpose | solution.py:19
  90.4 28.5 %all-gather.11.cloned.1.call-done = bf16[1024,2048]{1,0:T(8,128)(2,1)} async-done(((bf16[1024,256]{1,0:T(8,128)(2,1)}), bf16[1024,2048]{1,0:T(8,128)(2,1)}) %all-gather.11.cloned.1.call-update) | async-done | bytes 4194320 | tf_op jit(solution)/shard_map/all_gather | solution.py:24
  118.9 3.7 %fusion.1 = f32[1024,256]{1,0:T(8,128)S(1)} fusion(bf16[1024,2048]{1,0:T(8,128)(2,1)} %all-gather.11.cloned.1.call-done, bf16[8,2048,256]{2,1,0:T(8,128)(2,1)} %bitcast.44), kind=kOutput, calls=%fused_computation.16 | convolution fusion | flops 1073741824 | bytes 6291456 | tf_op jit(solution)/shard_map/dot_general | solution.py:25
  122.6 33.8 %all-gather.13.cloned.1.call-done = bf16[1024,2048]{1,0:T(8,128)(2,1)} async-done(((bf16[1024,256]{1,0:T(8,128)(2,1)}), bf16[1024,2048]{1,0:T(8,128)(2,1)}) %all-gather.13.cloned.1.call-update) | async-done | bytes 4194320 | tf_op jit(solution)/shard_map/all_gather | solution.py:24
  156.4 3.7 %convolution_add_fusion = f32[1024,256]{1,0:T(8,128)S(1)} fusion(f32[1024,256]{1,0:T(8,128)S(1)} %fusion.1, bf16[1024,2048]{1,0:T(8,128)(2,1)} %all-gather.13.cloned.1.call-done, bf16[8,2048,256]{2,1,0:T(8,128)(2,1)} %bitcast.45), kind=kOutput, calls=%fused_computation | convolution fusion | flops 1074003968 | bytes 7340032 | tf_op jit(solution)/shard_map/dot_general | solution.py:25
  160.1 29.2 %all-gather.15.cloned.1.call-done = bf16[768,2048]{1,0:T(8,128)(2,1)} async-done(((bf16[768,256]{1,0:T(8,128)(2,1)}), bf16[768,2048]{1,0:T(8,128)(2,1)}) %all-gather.15.cloned.1.call-update) | async-done | bytes 3145744 | tf_op jit(solution)/shard_map/all_gather | solution.py:24
  189.4 3.2 convolution_add_fusion.2
  192.5 0.1 constant_dynamic-update-slice_fusion.4
  192.6 29.8 %all-gather.17.cloned.1.call-done = bf16[768,2048]{1,0:T(8,128)(2,1)} async-done(((bf16[768,256]{1,0:T(8,128)(2,1)}), bf16[768,2048]{1,0:T(8,128)(2,1)}) %all-gather.17.cloned.1.call-update) | async-done | bytes 3145744 | tf_op jit(solution)/shard_map/all_gather | solution.py:24
  222.3 3.2 constant_dynamic-update-slice_fusion.3
  225.5 25.7 %all-gather.19.cloned.1.call-done = bf16[512,2048]{1,0:T(8,128)(2,1)} async-done(((bf16[512,256]{1,0:T(8,128)(2,1)}), bf16[512,2048]{1,0:T(8,128)(2,1)}) %all-gather.19.cloned.1.call-update) | async-done | bytes 2097168 | tf_op jit(solution)/shard_map/all_gather | solution.py:24
  251.2 2.6 constant_dynamic-update-slice_fusion.2
  253.8 26.4 %all-gather.21.cloned.1.call-done = bf16[512,2048]{1,0:T(8,128)(2,1)} async-done(((bf16[512,256]{1,0:T(8,128)(2,1)}), bf16[512,2048]{1,0:T(8,128)(2,1)}) %all-gather.21.cloned.1.call-update) | async-done | bytes 2097168 | tf_op jit(solution)/shard_map/all_gather | solution.py:24
  280.2 2.6 constant_dynamic-update-slice_fusion.1
  282.8 23.2 %all-gather.23.cloned.1.call-done = bf16[256,2048]{1,0:T(8,128)(2,1)} async-done(((bf16[256,256]{1,0:T(8,128)(2,1)}), bf16[256,2048]{1,0:T(8,128)(2,1)}) %all-gather.23.cloned.1.call-update) | async-done | bytes 1048592 | tf_op jit(solution)/shard_map/all_gather | solution.py:24
  306.0 2.0 constant_dynamic-update-slice_fusion
  308.0 23.8 %all-gather.25.cloned.1.call-done = bf16[256,2048]{1,0:T(8,128)(2,1)} async-done(((bf16[256,256]{1,0:T(8,128)(2,1)}), bf16[256,2048]{1,0:T(8,128)(2,1)}) %all-gather.25.cloned.1.call-update) | async-done | bytes 1048592 | tf_op jit(solution)/shard_map/all_gather | solution.py:24
  331.7 2.0 fusion
  333.7 0.8 convert_element_type.3
  (10 shorter events, 0.3 us)
Async XLA Ops:
  6.5 76.2 %all-gather.27.cloned.1.call-start = ((), (), s32[]{:S(2)}) async-start(), calls=%async_computation.8 | async-start | bytes 8912896 | tf_op jit(solution)/shard_map/all_gather | solution.py:18
  7.3 111.6 %all-gather.11.cloned.1.call-start = ((), (), s32[]{:S(2)}) async-start(), calls=%async_computation | async-start | bytes 4718592 | tf_op jit(solution)/shard_map/all_gather | solution.py:24
  9.6 146.8 %all-gather.13.cloned.1.call-start = ((), (), s32[]{:S(2)}) async-start(), calls=%async_computation.1 | async-start | bytes 4718592 | tf_op jit(solution)/shard_map/all_gather | solution.py:24
  10.3 179.0 %all-gather.15.cloned.1.call-start = ((), (), s32[]{:S(2)}) async-start(), calls=%async_computation.2 | async-start | bytes 3538944 | tf_op jit(solution)/shard_map/all_gather | solution.py:24
  12.5 209.9 %all-gather.17.cloned.1.call-start = ((), (), s32[]{:S(2)}) async-start(), calls=%async_computation.3 | async-start | bytes 3538944 | tf_op jit(solution)/shard_map/all_gather | solution.py:24
  13.0 238.2 %all-gather.19.cloned.1.call-start = ((), (), s32[]{:S(2)}) async-start(), calls=%async_computation.4 | async-start | bytes 2359296 | tf_op jit(solution)/shard_map/all_gather | solution.py:24
  15.0 265.2 %all-gather.21.cloned.1.call-start = ((), (), s32[]{:S(2)}) async-start(), calls=%async_computation.5 | async-start | bytes 2359296 | tf_op jit(solution)/shard_map/all_gather | solution.py:24
  15.7 290.2 %all-gather.23.cloned.1.call-start = ((), (), s32[]{:S(2)}) async-start(), calls=%async_computation.6 | async-start | bytes 1179648 | tf_op jit(solution)/shard_map/all_gather | solution.py:24
  17.5 314.2 %all-gather.25.cloned.1.call-start = ((), (), s32[]{:S(2)}) async-start(), calls=%async_computation.7 | async-start | bytes 1179648 | tf_op jit(solution)/shard_map/all_gather | solution.py:24
Sparse Core Ops, SparseCore 0:
  9.5 73.2 all-gather.26
  84.4 34.3 all-gather.10
  120.6 35.7 all-gather.12
  157.9 31.4 all-gather.14
  190.9 31.4 all-gather.16
  223.9 27.2 all-gather.18
  252.9 27.2 all-gather.20
  281.9 24.0 all-gather.22
  307.7 24.0 all-gather.24
where the time goes:
time: 342 us; the launch traced here: 341 us
  waiting for transfers between devices  288 us (84%)
  matrix products  22.9 us (7%)
  local copies, waits for them, and re-layouts  15.6 us (5%)
  between operations  13.3 us (4%)
    all_gather x8, waiting for transfers between devices, local_product(): panels = lax.all_gather(panel, 'col', axis=1, tiled=True)  220 us
    all_gather x1, waiting for transfers between devices, local_product(): gathered_rhs = lax.all_gather(rhs_loc, 'row', axis=0)  64.5 us
    dot_general x8, matrix products, local_product(): jnp.dot(panels, rhs_steps[step], preferred_element_type=jnp.float32)  22.9 us
    slice x4, local copies, waits for them, and re-layouts, local_product(): panel = lower_loc[first_row:, step * BLOCK_SIZE:(step + 1) * BLOCK_SIZE]  7.92 us
    transpose x1, local copies, waits for them, and re-layouts, local_product(): gathered_rhs.reshape(grid_rows, row_blocks, BLOCK_SIZE, rhs_cols)  7.63 us
  transfers between devices with their start and end apart: 9, of which 9 were waited for; matrix products, arithmetic and copies ran while one was open for 11% of the time, Pallas kernels for 0%

commit v1 on v0

v1 whole, which is shorter than its diff:
```python
import jax
import jax.numpy as jnp
from jax import lax
from jax.experimental import pallas as pl
from jax.experimental.pallas import tpu as pltpu
from jax.sharding import PartitionSpec as P

BLOCK = 256
HALF = 128
STAGES = 8
SLABS = 4
MESH = pl.DeviceIdType.MESH
F32 = jnp.float32


def _rem4(v):
    return lax.rem(v + 8, 4)


def _kernel(l_hbm, b_hbm, out_ref, l_all, b_all, acc, relay_lo, relay_hi, from_lo, from_hi,
            l_loc_sem, l_send_sem, l_recv_sem, b_send, b_recv, r_send, r_recv):
    row = lax.axis_index("row")
    col = lax.axis_index("col")
    z, y = row // 4, lax.rem(row, 4)
    x, core = col // 2, lax.rem(col, 2)

    def dev(zz, yy, xx, cc=None):
        return {"row": zz * 4 + yy, "col": xx * 2 + (core if cc is None else cc)}

    z_lo, z_hi = dev(_rem4(z - 1), y, x), dev(_rem4(z + 1), y, x)
    y_lo, y_hi = dev(z, _rem4(y - 1), x), dev(z, _rem4(y + 1), x)
    x_lo, x_hi = dev(z, y, _rem4(x - 1)), dev(z, y, _rem4(x + 1))
    partner = dev(z, y, x, 1 - core)

    def root_info(zt, yt):
        dz = _rem4(zt - x // 2)
        dy = _rem4(yt - 2 * lax.rem(x, 2) + 1)
        off_z, blk = lax.rem(dz, 2), dz // 2
        par, off_y = dy // 2, 1 - lax.rem((dy + 1) // 2, 2)
        return off_z, blk, par, off_y

    def unit(kind, zt, yt):
        off_z, blk, par, off_y = root_info(zt, yt)
        if kind == 0:
            return blk * 256 + par * HALF, (2 * off_z + off_y) * HALF
        return 512 + par * 256 + blk * HALF, (2 * off_y + off_z) * HALF

    def region(kind, zt, yt):
        off_z, blk, par, off_y = root_info(zt, yt)
        if kind == 0:
            return blk * 256, off_z * 256
        return 512 + par * 256, off_y * 256

    tgt_x = 2 * lax.rem(z, 2) + y // 2
    own_par = lax.rem(y, 2)

    def target(kind):
        hi, lo = x // 2, lax.rem(x, 2)
        off_z, off_y = (hi, lo) if kind == 0 else (lo, hi)
        return _rem4(z + off_z), _rem4(y + (2 * own_par - 1) * off_y)

    def source(kind):
        off_z, blk, par, off_y = root_info(z, y)
        xs = 2 * off_z + off_y if kind == 0 else 2 * off_y + off_z
        return dev(x // 2 + 2 * blk, 2 * lax.rem(x, 2) + par, xs)

    targets = [target(0), target(1)]
    to_self = [jnp.logical_and(jnp.logical_and(zt == z, yt == y), tgt_x == x) for zt, yt in targets]

    def slab_cols(ab, blk, par):
        return ab * 512 + (blk * 256 + par * HALF if ab == 0 else par * 256 + blk * HALF)

    def slab_copies(s):
        for ab in range(2):
            for blk in range(2):
                src = l_hbm.at[pl.ds(s * BLOCK, 1024 - s * BLOCK), pl.ds((2 * s + blk) * BLOCK + ab * HALF, HALF)]
                step = 256 if ab else HALF
                dst_col = pl.multiple_of(slab_cols(ab, blk, 0) + core * step, HALF)
                dst = l_all.at[s, pl.ds(s * BLOCK, 1024 - s * BLOCK), pl.ds(dst_col, HALF)]
                yield 2 * ab + blk, src, dst

    for s in range(SLABS):
        for i, src, dst in slab_copies(s):
            pltpu.make_async_copy(src, dst, l_loc_sem.at[s, i]).start()

    barrier = pltpu.get_barrier_semaphore()
    for d in (z_lo, z_hi, y_lo, y_hi, x_lo, x_hi, partner, source(0), source(1)):
        pl.semaphore_signal(barrier, inc=1, device_id=d, device_id_type=MESH)
    pl.semaphore_wait(barrier, 9)

    sends = []

    def send(src, dst, s_sem, r_sem, where):
        cp = pltpu.make_async_remote_copy(src_ref=src, dst_ref=dst, send_sem=s_sem, recv_sem=r_sem,
                                          device_id=where, device_id_type=MESH)
        cp.start()
        sends.append(cp)

    def arrived(ref, sem):
        pltpu.make_async_copy(ref, ref, sem).wait()

    def home_piece(t, kind):
        s, h = t // 2, t % 2
        src = b_hbm.at[pl.ds(s * BLOCK + kind * HALF, HALF), pl.ds(h * HALF, HALF)]
        blk, par = z // 2, own_par
        r0 = blk * 256 + par * HALF if kind == 0 else 512 + par * 256 + blk * HALF
        dst = b_all.at[t, pl.ds(pl.multiple_of(r0, HALF), HALF), pl.ds(pl.multiple_of(x * HALF, HALF), HALF)]
        return src, dst

    def root_copy(t, kind):
        src, dst = home_piece(t, kind)
        zt, yt = targets[kind]
        return pltpu.make_async_remote_copy(src_ref=src, dst_ref=dst, send_sem=b_send.at[t, kind], recv_sem=b_recv.at[t, kind],
                                            device_id=dev(zt, yt, tgt_x), device_id_type=MESH)

    for kind in range(2):
        @pl.when(jnp.logical_not(to_self[kind]))
        def _():
            for t in range(STAGES):
                root_copy(t, kind).start()

        @pl.when(to_self[kind])
        def _():
            for t in range(STAGES):
                src, dst = home_piece(t, kind)
                pltpu.make_async_copy(src, dst, b_recv.at[t, kind]).start()

    for s in range(SLABS):
        for i, src, dst in slab_copies(s):
            send(src, dst, l_send_sem.at[s, i], l_recv_sem.at[s, i], partner)

    def unit_ref(t, kind, zt, yt):
        r0, c0 = unit(kind, zt, yt)
        return b_all.at[t, pl.ds(pl.multiple_of(r0, HALF), HALF), pl.ds(pl.multiple_of(c0, HALF), HALF)]

    def region_ref(t, kind, zt, yt):
        r0, c0 = region(kind, zt, yt)
        return b_all.at[t, pl.ds(pl.multiple_of(r0, 256), 256), pl.ds(pl.multiple_of(c0, 256), 256)]

    lo_pos = [(z, _rem4(y - 1)), (_rem4(z - 1), y)]
    hi_pos = [(z, _rem4(y + 1)), (_rem4(z + 1), y)]
    lo_dev, hi_dev = [y_lo, z_lo], [y_hi, z_hi]
    any_unit = b_all.at[0, pl.ds(0, HALF), pl.ds(0, HALF)]
    any_region = b_all.at[0, pl.ds(0, 256), pl.ds(0, 256)]

    def gather_own(t, kind, phase):
        axis = kind if phase == 0 else 1 - kind
        ref = unit_ref(t, kind, z, y) if phase == 0 else region_ref(t, kind, z, y)
        base = 2 + 6 * kind + 3 * phase
        send(ref, ref, b_send.at[t, base], b_recv.at[t, base], hi_dev[axis])
        send(ref, ref, b_send.at[t, base + 1], b_recv.at[t, base + 1], lo_dev[axis])

    def gather_relay(t, kind, phase):
        axis = kind if phase == 0 else 1 - kind
        up = (t + kind + phase) % 2 == 0
        pos = lo_pos[axis] if up else hi_pos[axis]
        base = 2 + 6 * kind + 3 * phase
        arrived(any_unit if phase == 0 else any_region, b_recv.at[t, base if up else base + 1])
        ref = unit_ref(t, kind, *pos) if phase == 0 else region_ref(t, kind, *pos)
        send(ref, ref, b_send.at[t, base + 2], b_recv.at[t, base + 2], hi_dev[axis] if up else lo_dev[axis])

    def gather_rest(t, kind, phase):
        up = (t + kind + phase) % 2 == 0
        base = 2 + 6 * kind + 3 * phase
        ref = any_unit if phase == 0 else any_region
        arrived(ref, b_recv.at[t, base + 1 if up else base])
        arrived(ref, b_recv.at[t, base + 2])

    def first_own(t):
        for kind in range(2):
            arrived(any_unit, b_recv.at[t, kind])
            gather_own(t, kind, 0)

    def first_relay(t):
        for kind in range(2):
            gather_relay(t, kind, 0)

    def second_own(t):
        for kind in range(2):
            gather_rest(t, kind, 0)
            gather_own(t, kind, 1)

    def second_relay(t):
        for kind in range(2):
            gather_relay(t, kind, 1)

    def product(t, sp):
        s, h = t // 2, t % 2
        lhs = l_all[s, sp * BLOCK:(sp + 1) * BLOCK, :]
        for n in range(2):
            p = jnp.dot(lhs, b_all[t, :, n * 256:(n + 1) * 256], preferred_element_type=F32)
            for j in range(2):
                part = p[:, j * HALF:(j + 1) * HALF]
                if s > 0:
                    part = part + acc[sp, h, 2 * n + j]
                acc[sp, h, 2 * n + j] = part

    def compute(t):
        s = t // 2
        for kind in range(2):
            gather_rest(t, kind, 1)
        if t % 2 == 0:
            for i in range(4):
                arrived(l_all.at[s, pl.ds(s * BLOCK, 1024 - s * BLOCK), pl.ds(0, HALF)], l_loc_sem.at[s, i])
                arrived(l_all.at[s, pl.ds(s * BLOCK, 1024 - s * BLOCK), pl.ds(0, HALF)], l_recv_sem.at[s, i])
        product(t, s)

    def part_ref(t, slot, half):
        return acc.at[t // 2, t % 2, slot, pl.ds(half * HALF, HALF), :]

    xp1, xm1, xp2 = _rem4(x + 1), _rem4(x - 1), _rem4(x + 2)

    def reduce_first(t):
        send(part_ref(t, xp2, 0), relay_lo.at[t], r_send.at[t, 0], r_recv.at[t, 0], x_hi)
        send(part_ref(t, xp2, 1), relay_hi.at[t], r_send.at[t, 1], r_recv.at[t, 1], x_lo)
        send(part_ref(t, xp1, 1), from_lo.at[t, pl.ds(HALF, HALF), :], r_send.at[t, 2], r_recv.at[t, 2], x_hi)
        send(part_ref(t, xm1, 0), from_hi.at[t, pl.ds(0, HALF), :], r_send.at[t, 3], r_recv.at[t, 3], x_lo)

    def reduce_second(t):
        s, h = t // 2, t % 2
        arrived(relay_lo.at[t], r_recv.at[t, 0])
        acc[s, h, xp1, 0:HALF, :] = acc[s, h, xp1, 0:HALF, :] + relay_lo[t]
        send(part_ref(t, xp1, 0), from_lo.at[t, pl.ds(0, HALF), :], r_send.at[t, 4], r_recv.at[t, 4], x_hi)
        arrived(relay_hi.at[t], r_recv.at[t, 1])
        acc[s, h, xm1, HALF:BLOCK, :] = acc[s, h, xm1, HALF:BLOCK, :] + relay_hi[t]
        send(part_ref(t, xm1, 1), from_hi.at[t, pl.ds(HALF, HALF), :], r_send.at[t, 5], r_recv.at[t, 5], x_lo)

    def finish(t):
        s, h = t // 2, t % 2
        for i in (2, 3, 4, 5):
            arrived(relay_lo.at[t], r_recv.at[t, i])
        total = acc[s, h, x] + from_lo[t] + from_hi[t]
        out_ref[s * BLOCK:(s + 1) * BLOCK, h * HALF:(h + 1) * HALF] = total.astype(out_ref.dtype)

    for i in range(STAGES + 6):
        if i < STAGES:
            first_own(i)
        if 0 <= i - 1 < STAGES:
            first_relay(i - 1)
        if 0 <= i - 2 < STAGES:
            second_own(i - 2)
        if 0 <= i - 3 < STAGES:
            second_relay(i - 3)
        if 0 <= i - 4 < STAGES:
            compute(i - 4)
            reduce_first(i - 4)
        if 0 <= i - 5 < STAGES:
            reduce_second(i - 5)
        if 0 <= i - 4 < STAGES:
            for sp in range((i - 4) // 2 + 1, SLABS):
                product(i - 4, sp)
        if 0 <= i - 6 < STAGES:
            finish(i - 6)

    for cp in sends:
        cp.wait_send()
    for kind in range(2):
        @pl.when(jnp.logical_not(to_self[kind]))
        def _():
            for t in range(STAGES):
                root_copy(t, kind).wait_send()


def solution(mesh):
    def local_product(lower_loc, rhs_loc):
        rows, cols = rhs_loc.shape
        bf16 = lower_loc.dtype
        return pl.pallas_call(
            _kernel,
            out_shape=jax.ShapeDtypeStruct((rows, cols), bf16),
            in_specs=[pl.BlockSpec(memory_space=pl.ANY)] * 2,
            out_specs=pl.BlockSpec(memory_space=pltpu.VMEM),
            scratch_shapes=[
                pltpu.VMEM((SLABS, 1024, 1024), bf16),
                pltpu.VMEM((STAGES, 1024, 512), bf16),
                pltpu.VMEM((SLABS, 2, 4, BLOCK, HALF), F32),
                pltpu.VMEM((STAGES, HALF, HALF), F32),
                pltpu.VMEM((STAGES, HALF, HALF), F32),
                pltpu.VMEM((STAGES, BLOCK, HALF), F32),
                pltpu.VMEM((STAGES, BLOCK, HALF), F32),
                pltpu.SemaphoreType.DMA((SLABS, 4)),
                pltpu.SemaphoreType.DMA((SLABS, 4)),
                pltpu.SemaphoreType.DMA((SLABS, 4)),
                pltpu.SemaphoreType.DMA((STAGES, 14)),
                pltpu.SemaphoreType.DMA((STAGES, 14)),
                pltpu.SemaphoreType.DMA((STAGES, 6)),
                pltpu.SemaphoreType.DMA((STAGES, 6)),
            ],
            compiler_params=pltpu.CompilerParams(collective_id=0, has_side_effects=True, vmem_limit_bytes=48 * 1024 * 1024),
        )(lower_loc, rhs_loc)

    return jax.shard_map(local_product, mesh=mesh, in_specs=(P("row", "col"), P("row", ("batch", "col"))), out_specs=P("row", ("batch", "col")), check_vma=False)
```

time: 342 us -> 95.4 us (0.28)
  waiting for transfers between devices: 288 us -> 0 us
  Pallas kernels: 0 us -> 91.2 us
  matrix products: 22.9 us -> 0 us
  between operations: 13.3 us -> 0.01 us
  local copies, waits for them, and re-layouts: 15.6 us -> 4.02 us
    all_gather x9 -> x0, waiting for transfers between devices: 285 us -> none  [the longest x8 220 us: local_product(): panels = lax.all_gather(panel, 'col', axis=1, tiled=True)]
    pallas_call x0 -> x1, Pallas kernels: none -> 91.2 us  [local_product(): pl.pallas_call(_kernel, out_shape=jax.ShapeDtypeStruct((rows, cols), bf16...]
    dot_general x8 -> x0, matrix products: 22.9 us -> none  [local_product(): jnp.dot(panels, rhs_steps[step], preferred_element_type=jnp.float32)]
    slice x4 -> x0, local copies, waits for them, and re-layouts: 7.92 us -> none  [local_product(): panel = lower_loc[first_row:, step * BLOCK_SIZE:(step + 1) * BLOCK_SIZE]]
    transpose x1 -> x0, local copies, waits for them, and re-layouts: 7.63 us -> none  [local_product(): gathered_rhs.reshape(grid_rows, row_blocks, BLOCK_SIZE, rhs_cols)]
    unnamed x0 -> x5, local copies, waits for them, and re-layouts: none -> 4.02 us
  transfers between devices with their start and end apart: 9 -> 0, of which waited for: 9 -> 0; matrix products, arithmetic and copies ran while one was open for 11% -> 0% of each run, Pallas kernels for 0% -> 0%
where the time goes in v1:
time: 95.4 us; the launch traced here: 95.2 us
  Pallas kernels  91.2 us (96%)
  local copies, waits for them, and re-layouts  4.02 us (4%)
    pallas_call x1, Pallas kernels, local_product(): pl.pallas_call(_kernel, out_shape=jax.ShapeDtypeStruct((rows, cols), bf16...  91.2 us
    unnamed x5, local copies, waits for them, and re-layouts  4.02 us

profile of v1, /device:TPU:0, one launch (start us, length us, event | category | flops | bytes accessed | tf_op | source)
XLA Modules:
  0.0 95.2 jit_solution(16630315727562146362)
XLA Ops:
  0.0 0.0 copy-start
  0.0 2.2 %copy-done = bf16[1024,2048]{1,0:T(8,128)(2,1)S(1)} copy-done((bf16[1024,2048]{1,0:T(8,128)(2,1)S(1)}, bf16[1024,2048]{1,0:T(8,128)(2,1)}, u32[]{:S(2)}) %copy-start) | copy-done | bytes 4194328
  2.2 0.0 copy-start.1
  2.2 1.0 %copy-done.1 = bf16[1024,256]{1,0:T(8,128)(2,1)S(1)} copy-done((bf16[1024,256]{1,0:T(8,128)(2,1)S(1)}, bf16[1024,256]{1,0:T(8,128)(2,1)}, u32[]{:S(2)}) %copy-start.1) | copy-done | bytes 524312
  3.2 91.2 %shard_map.28 = bf16[1024,256]{1,0:T(8,128)(2,1)S(1)} custom-call(bf16[1024,2048]{1,0:T(8,128)(2,1)S(1)} %copy-done, bf16[1024,256]{1,0:T(8,128)(2,1)S(1)} %copy-done.1), custom_call_target="tpu_custom_call" | custom-call | tf_op jit(solution)/shard_map/pallas_call | solution.py:268
  94.4 0.8 copy.4
Async XLA Ops:
  0.0 2.2 %copy-start = (bf16[1024,2048]{1,0:T(8,128)(2,1)S(1)}, bf16[1024,2048]{1,0:T(8,128)(2,1)}, u32[]{:S(2)}) copy-start(bf16[1024,2048]{1,0:T(8,128)(2,1)} %l_hbm.1) | copy-start | bytes 12582916
  2.2 1.0 %copy-start.1 = (bf16[1024,256]{1,0:T(8,128)(2,1)S(1)}, bf16[1024,256]{1,0:T(8,128)(2,1)}, u32[]{:S(2)}) copy-start(bf16[1024,256]{1,0:T(8,128)(2,1)} %b_hbm.1) | copy-start | bytes 1572868

commit v2 on v1

v2 whole, which is shorter than its diff:
```python
import jax
import jax.numpy as jnp
from jax import lax
from jax.experimental import pallas as pl
from jax.experimental.pallas import tpu as pltpu
from jax.sharding import PartitionSpec as P

BLOCK = 256
HALF = 128
STAGES = 8
SLABS = 4
MESH = pl.DeviceIdType.MESH
F32 = jnp.float32
MOVE_FIRST = 2
ORDER = (("move", -2), ("enter", -1), ("own1", 0), ("relay1", 1), ("own2", 2), ("relay2", 3), ("compute", 4), ("reduce1", 4),
         ("reduce2", 5), ("others", 4), ("finish", 6))


def _rem4(v):
    return lax.rem(v + 8, 4)


def _kernel(l_hbm, b_hbm, out_ref, l_all, b_all, acc, relay_lo, relay_hi, from_lo, from_hi,
            l_loc_sem, l_send_sem, l_recv_sem, b_send, b_recv, r_send, r_recv, staged, m_send, m_recv):
    row = lax.axis_index("row")
    col = lax.axis_index("col")
    z, y = row // 4, lax.rem(row, 4)
    x, core = col // 2, lax.rem(col, 2)

    def dev(zz, yy, xx, cc=None):
        return {"row": zz * 4 + yy, "col": xx * 2 + (core if cc is None else cc)}

    z_lo, z_hi = dev(_rem4(z - 1), y, x), dev(_rem4(z + 1), y, x)
    y_lo, y_hi = dev(z, _rem4(y - 1), x), dev(z, _rem4(y + 1), x)
    x_lo, x_hi = dev(z, y, _rem4(x - 1)), dev(z, y, _rem4(x + 1))
    partner = dev(z, y, x, 1 - core)

    def offsets(kind, h, xs):
        v = 3 - xs if h else xs
        hi, lo = v // 2, lax.rem(v, 2)
        return (hi, lo) if kind == 0 else (lo, hi)

    def moved(kind, back, zz, yy, off_z, off_y):
        dz = off_z if (kind == 0) != back else -off_z
        return _rem4(zz + dz), _rem4(yy + (2 * lax.rem(yy, 2) - 1) * off_y)

    def plane_of(zz, yy):
        return 2 * lax.rem(zz, 2) + yy // 2

    def root_info(kind, zt, yt):
        dz = _rem4(zt - x // 2)
        dy = _rem4(yt - 2 * lax.rem(x, 2) + 1)
        off_z = lax.rem(dz, 2)
        blk = dz // 2 if kind == 0 else lax.rem((dz + 1) // 2, 2)
        par, off_y = dy // 2, 1 - lax.rem((dy + 1) // 2, 2)
        return off_z, blk, par, off_y

    def slab_copy(s):
        rows = pl.ds(s * BLOCK, 1024 - s * BLOCK)
        return l_hbm.at[rows, pl.ds(s * 512, 512)], l_all.at[s, rows, pl.ds(pl.multiple_of(core * 512, 512), 512)]

    for s in range(SLABS):
        src, dst = slab_copy(s)
        pltpu.make_async_copy(src, dst, l_loc_sem.at[s]).start()

    barrier = pltpu.get_barrier_semaphore()
    y_side = _rem4(y + 2 * lax.rem(y, 2) - 1)
    for d in (z_lo, z_hi, y_lo, y_hi, x_lo, x_hi, dev(z, y, _rem4(x + 2)), partner,
              dev(_rem4(z - 1), y_side, x), dev(_rem4(z + 1), y_side, x)):
        pl.semaphore_signal(barrier, inc=1, device_id=d, device_id_type=MESH)
    pl.semaphore_wait(barrier, 10)

    sends = []

    def send(src, dst, s_sem, r_sem, where):
        cp = pltpu.make_async_remote_copy(src_ref=src, dst_ref=dst, send_sem=s_sem, recv_sem=r_sem,
                                          device_id=where, device_id_type=MESH)
        cp.start()
        sends.append(cp)

    def arrived(ref, sem):
        pltpu.make_async_copy(ref, ref, sem).wait()

    in_plane = plane_of(z, y) == x

    def final_ref(t, kind, zs, ys, xs):
        return b_all.at[t, lax.rem(ys, 2), zs // 2, kind, :, pl.ds(pl.multiple_of(xs * HALF, HALF), HALF)]

    def move_copies(t, kind):
        s, h = t // 2, t % 2
        src = b_hbm.at[pl.ds(s * BLOCK + kind * HALF, HALF), pl.ds(h * HALF, HALF)]
        off_z, off_y = offsets(kind, h, x)
        zt, yt = moved(kind, False, z, y, off_z, off_y)
        stay = x == (3 if h else 0)
        for direct in (True, False):
            dst = final_ref(t, kind, z, y, x) if direct else staged.at[t, kind]
            sem = (b_recv if direct else m_recv).at[t, kind]
            cond = in_plane if direct else jnp.logical_not(in_plane)
            yield (jnp.logical_and(cond, stay), pltpu.make_async_copy(src, dst, sem), False)
            yield (jnp.logical_and(cond, jnp.logical_not(stay)),
                   pltpu.make_async_remote_copy(src_ref=src, dst_ref=dst, send_sem=m_send.at[t, kind], recv_sem=sem,
                                                device_id=dev(zt, yt, x), device_id_type=MESH), True)

    def move(t):
        for kind in range(2):
            for cond, cp, _ in move_copies(t, kind):
                pl.when(cond)(cp.start)

    def enter_copy(t, kind):
        off_z, off_y = offsets(kind, t % 2, x)
        zs, ys = moved(kind, True, z, y, off_z, off_y)
        xt = plane_of(zs, ys)
        cp = pltpu.make_async_remote_copy(src_ref=staged.at[t, kind], dst_ref=final_ref(t, kind, zs, ys, x),
                                          send_sem=b_send.at[t, kind], recv_sem=b_recv.at[t, kind],
                                          device_id=dev(z, y, xt), device_id_type=MESH)
        return xt != x, cp

    def enter(t):
        for kind in range(2):
            cond, cp = enter_copy(t, kind)

            @pl.when(cond)
            def _():
                arrived(staged.at[t, kind], m_recv.at[t, kind])
                cp.start()

    for t in range(MOVE_FIRST):
        move(t)

    for s in range(SLABS):
        src, dst = slab_copy(s)
        send(src, dst, l_send_sem.at[s], l_recv_sem.at[s], partner)

    def unit_ref(t, kind, zt, yt):
        off_z, blk, par, off_y = root_info(kind, zt, yt)
        v = 2 * off_z + off_y if kind == 0 else 2 * off_y + off_z
        xs = 3 - v if t % 2 else v
        return b_all.at[t, par, blk, kind, :, pl.ds(pl.multiple_of(xs * HALF, HALF), HALF)]

    def region_ref(t, kind, zt, yt):
        off_z, blk, par, off_y = root_info(kind, zt, yt)
        pair = off_z if kind == 0 else off_y
        cols = pl.ds(pl.multiple_of((1 - pair if t % 2 else pair) * 256, 256), 256)
        if kind == 0:
            return b_all.at[t, :, blk, 0, :, cols]
        return b_all.at[t, par, :, 1, :, cols]

    lo_pos = [(z, _rem4(y - 1)), (_rem4(z - 1), y)]
    hi_pos = [(z, _rem4(y + 1)), (_rem4(z + 1), y)]
    lo_dev, hi_dev = [y_lo, z_lo], [y_hi, z_hi]
    any_unit = b_all.at[0, 0, 0, 0, :, pl.ds(0, HALF)]
    any_region = b_all.at[0, 0, :, 0, :, pl.ds(0, 256)]

    def gather_own(t, kind, phase):
        axis = kind if phase == 0 else 1 - kind
        ref = unit_ref(t, kind, z, y) if phase == 0 else region_ref(t, kind, z, y)
        base = 2 + 6 * kind + 3 * phase
        send(ref, ref, b_send.at[t, base], b_recv.at[t, base], hi_dev[axis])
        send(ref, ref, b_send.at[t, base + 1], b_recv.at[t, base + 1], lo_dev[axis])

    def gather_relay(t, kind, phase):
        axis = kind if phase == 0 else 1 - kind
        up = (t + kind + phase) % 2 == 0
        pos = lo_pos[axis] if up else hi_pos[axis]
        base = 2 + 6 * kind + 3 * phase
        arrived(any_unit if phase == 0 else any_region, b_recv.at[t, base if up else base + 1])
        ref = unit_ref(t, kind, *pos) if phase == 0 else region_ref(t, kind, *pos)
        send(ref, ref, b_send.at[t, base + 2], b_recv.at[t, base + 2], hi_dev[axis] if up else lo_dev[axis])

    def gather_rest(t, kind, phase):
        up = (t + kind + phase) % 2 == 0
        base = 2 + 6 * kind + 3 * phase
        ref = any_unit if phase == 0 else any_region
        arrived(ref, b_recv.at[t, base + 1 if up else base])
        arrived(ref, b_recv.at[t, base + 2])

    def first_own(t):
        for kind in range(2):
            arrived(any_unit, b_recv.at[t, kind])
            gather_own(t, kind, 0)

    def first_relay(t):
        for kind in range(2):
            gather_relay(t, kind, 0)

    def second_own(t):
        for kind in range(2):
            gather_rest(t, kind, 0)
            gather_own(t, kind, 1)

    def second_relay(t):
        for kind in range(2):
            gather_relay(t, kind, 1)

    def product(t, sp):
        s, h = t // 2, t % 2
        lhs = l_all[s, sp * BLOCK:(sp + 1) * BLOCK, :]
        for n in range(2):
            rhs = b_all[t, :, :, :, :, n * 256:(n + 1) * 256].reshape(1024, 256)
            p = jnp.dot(lhs, rhs, preferred_element_type=F32)
            for j in range(2):
                part = p[:, j * HALF:(j + 1) * HALF]
                if s > 0:
                    part = part + acc[sp, h, 2 * n + j]
                acc[sp, h, 2 * n + j] = part

    def compute(t):
        s = t // 2
        for kind in range(2):
            gather_rest(t, kind, 1)
        if t % 2 == 0:
            for sem in (l_loc_sem, l_recv_sem):
                arrived(l_all.at[s, pl.ds(s * BLOCK, 1024 - s * BLOCK), pl.ds(0, 512)], sem.at[s])
        product(t, s)

    def part_ref(t, slot, half):
        return acc.at[t // 2, t % 2, slot, pl.ds(half * HALF, HALF), :]

    xp1, xm1, xp2 = _rem4(x + 1), _rem4(x - 1), _rem4(x + 2)

    def reduce_first(t):
        send(part_ref(t, xp2, 0), relay_lo.at[t], r_send.at[t, 0], r_recv.at[t, 0], x_hi)
        send(part_ref(t, xp2, 1), relay_hi.at[t], r_send.at[t, 1], r_recv.at[t, 1], x_lo)
        send(part_ref(t, xp1, 1), from_lo.at[t, pl.ds(HALF, HALF), :], r_send.at[t, 2], r_recv.at[t, 2], x_hi)
        send(part_ref(t, xm1, 0), from_hi.at[t, pl.ds(0, HALF), :], r_send.at[t, 3], r_recv.at[t, 3], x_lo)

    def reduce_second(t):
        s, h = t // 2, t % 2
        arrived(relay_lo.at[t], r_recv.at[t, 0])
        acc[s, h, xp1, 0:HALF, :] = acc[s, h, xp1, 0:HALF, :] + relay_lo[t]
        send(part_ref(t, xp1, 0), from_lo.at[t, pl.ds(0, HALF), :], r_send.at[t, 4], r_recv.at[t, 4], x_hi)
        arrived(relay_hi.at[t], r_recv.at[t, 1])
        acc[s, h, xm1, HALF:BLOCK, :] = acc[s, h, xm1, HALF:BLOCK, :] + relay_hi[t]
        send(part_ref(t, xm1, 1), from_hi.at[t, pl.ds(HALF, HALF), :], r_send.at[t, 5], r_recv.at[t, 5], x_lo)

    def finish(t):
        s, h = t // 2, t % 2
        for i in (2, 3, 4, 5):
            arrived(relay_lo.at[t], r_recv.at[t, i])
        total = acc[s, h, x] + from_lo[t] + from_hi[t]
        out_ref[s * BLOCK:(s + 1) * BLOCK, h * HALF:(h + 1) * HALF] = total.astype(out_ref.dtype)

    def others(t):
        for sp in range(t // 2 + 1, SLABS):
            product(t, sp)

    steps = {"move": move, "enter": enter, "own1": first_own, "relay1": first_relay, "own2": second_own, "relay2": second_relay,
             "compute": compute, "reduce1": reduce_first, "others": others, "reduce2": reduce_second, "finish": finish}
    for i in range(-4, STAGES + 8):
        for name, lag in ORDER:
            t = i - lag
            if 0 <= t < STAGES and not (name == "move" and t < MOVE_FIRST):
                steps[name](t)

    for cp in sends:
        cp.wait_send()
    for t in range(STAGES):
        for kind in range(2):
            for cond, cp, remote in move_copies(t, kind):
                if remote:
                    pl.when(cond)(cp.wait_send)
            cond, cp = enter_copy(t, kind)
            pl.when(cond)(cp.wait_send)


def solution(mesh):
    def local_product(lower_loc, rhs_loc):
        rows, cols = rhs_loc.shape
        bf16 = lower_loc.dtype
        return pl.pallas_call(
            _kernel,
            out_shape=jax.ShapeDtypeStruct((rows, cols), bf16),
            in_specs=[pl.BlockSpec(memory_space=pltpu.HBM)] * 2,
            out_specs=pl.BlockSpec(memory_space=pltpu.VMEM),
            scratch_shapes=[
                pltpu.VMEM((SLABS, 1024, 1024), bf16),
                pltpu.VMEM((STAGES, 2, 2, 2, HALF, 512), bf16),
                pltpu.VMEM((SLABS, 2, 4, BLOCK, HALF), F32),
                pltpu.VMEM((STAGES, HALF, HALF), F32),
                pltpu.VMEM((STAGES, HALF, HALF), F32),
                pltpu.VMEM((STAGES, BLOCK, HALF), F32),
                pltpu.VMEM((STAGES, BLOCK, HALF), F32),
                pltpu.SemaphoreType.DMA((SLABS,)),
                pltpu.SemaphoreType.DMA((SLABS,)),
                pltpu.SemaphoreType.DMA((SLABS,)),
                pltpu.SemaphoreType.DMA((STAGES, 14)),
                pltpu.SemaphoreType.DMA((STAGES, 14)),
                pltpu.SemaphoreType.DMA((STAGES, 6)),
                pltpu.SemaphoreType.DMA((STAGES, 6)),
                pltpu.VMEM((STAGES, 2, HALF, HALF), bf16),
                pltpu.SemaphoreType.DMA((STAGES, 2)),
                pltpu.SemaphoreType.DMA((STAGES, 2)),
            ],
            compiler_params=pltpu.CompilerParams(collective_id=0, has_side_effects=True, vmem_limit_bytes=63 * 1024 * 1024),
        )(lower_loc, rhs_loc)

    return jax.shard_map(local_product, mesh=mesh, in_specs=(P("row", "col"), P("row", ("batch", "col"))), out_specs=P("row", ("batch", "col")), check_vma=False)
```

time: 95.4 us -> 83 us (0.87)
  Pallas kernels: 91.2 us -> 80.9 us
  local copies, waits for them, and re-layouts: 4.02 us -> 1.87 us
    pallas_call x1, Pallas kernels: 91.2 us -> 80.9 us  [local_product(): pl.pallas_call(_kernel, out_shape=jax.ShapeDtypeStruct((rows, cols), bf16...]
    unnamed x5 -> x1, local copies, waits for them, and re-layouts: 4.02 us -> 1.87 us
where the time goes in v2:
time: 83 us; the launch traced here: 82.8 us
  Pallas kernels  80.9 us (97%)
  local copies, waits for them, and re-layouts  1.87 us (2%)
    pallas_call x1, Pallas kernels, local_product(): pl.pallas_call(_kernel, out_shape=jax.ShapeDtypeStruct((rows, cols), bf16...  80.9 us
    unnamed x1, local copies, waits for them, and re-layouts  1.87 us

profile of v2, /device:TPU:0, one launch (start us, length us, event | category | flops | bytes accessed | tf_op | source)
XLA Modules:
  0.0 82.8 jit_solution(14391670536155992654)
XLA Ops:
  0.0 80.9 %shard_map.28 = bf16[1024,256]{1,0:T(8,128)(2,1)} custom-call(bf16[1024,2048]{1,0:T(8,128)(2,1)} %l_hbm.1, bf16[1024,256]{1,0:T(8,128)(2,1)} %b_hbm.1), custom_call_target="tpu_custom_call" | custom-call | tf_op jit(solution)/shard_map/pallas_call | solution.py:270
  80.9 1.9 %copy.4 = bf16[1024,256]{1,0:T(8,128)(2,1)} copy(bf16[1024,256]{1,0:T(8,128)(2,1)} %shard_map.28) | data formatting | bytes 1048576

commit v3 on v2

v3 whole, which is shorter than its diff:
```python
import jax
import jax.numpy as jnp
from jax import lax
from jax.experimental import pallas as pl
from jax.experimental.pallas import tpu as pltpu
from jax.sharding import PartitionSpec as P

BLOCK = 256
HALF = 128
STAGES = 8
SLABS = 4
MESH = pl.DeviceIdType.MESH
F32 = jnp.float32
MOVE_FIRST = 8
ORDER = (("move", -2), ("enter", -1), ("own1", 0), ("relay1", 1), ("own2", 2), ("relay2", 3), ("compute", 4), ("reduce1", 4),
         ("reduce2", 5), ("others", 4), ("finish", 7))


def _rem4(v):
    return lax.rem(v + 8, 4)


def _kernel(l_hbm, b_hbm, out_ref, l_all, b_all, acc, relay_lo, relay_hi, from_lo, from_hi,
            staged, l_recv, m_recv, b_recv, r_recv, sent):
    row = lax.axis_index("row")
    col = lax.axis_index("col")
    z, y = row // 4, lax.rem(row, 4)
    x, core = col // 2, lax.rem(col, 2)

    def dev(zz, yy, xx, cc=None):
        return {"row": zz * 4 + yy, "col": xx * 2 + (core if cc is None else cc)}

    z_lo, z_hi = dev(_rem4(z - 1), y, x), dev(_rem4(z + 1), y, x)
    y_lo, y_hi = dev(z, _rem4(y - 1), x), dev(z, _rem4(y + 1), x)
    x_lo, x_hi = dev(z, y, _rem4(x - 1)), dev(z, y, _rem4(x + 1))
    partner = dev(z, y, x, 1 - core)

    def offsets(kind, h, xs):
        v = 3 - xs if h else xs
        hi, lo = v // 2, lax.rem(v, 2)
        return (hi, lo) if kind == 0 else (lo, hi)

    def moved(kind, back, zz, yy, off_z, off_y):
        dz = off_z if (kind == 0) != back else -off_z
        return _rem4(zz + dz), _rem4(yy + (2 * lax.rem(yy, 2) - 1) * off_y)

    def plane_of(zz, yy):
        return 2 * lax.rem(zz, 2) + yy // 2

    def root_info(kind, zt, yt):
        dz = _rem4(zt - x // 2)
        dy = _rem4(yt - 2 * lax.rem(x, 2) + 1)
        off_z = lax.rem(dz, 2)
        blk = dz // 2 if kind == 0 else lax.rem((dz + 1) // 2, 2)
        par, off_y = dy // 2, 1 - lax.rem((dy + 1) // 2, 2)
        return off_z, blk, par, off_y

    def slab_copy(s):
        rows = pl.ds(s * BLOCK, 1024 - s * BLOCK)
        return l_hbm.at[rows, pl.ds(s * 512, 512)], l_all.at[s, rows, pl.ds(pl.multiple_of(core * 512, 512), 512)]

    for s in range(SLABS):
        src, dst = slab_copy(s)
        pltpu.make_async_copy(src, dst, l_recv.at[s]).start()

    barrier = pltpu.get_barrier_semaphore()
    y_side = _rem4(y + 2 * lax.rem(y, 2) - 1)
    for d in (z_lo, z_hi, y_lo, y_hi, x_lo, x_hi, dev(z, y, _rem4(x + 2)), partner,
              dev(_rem4(z - 1), y_side, x), dev(_rem4(z + 1), y_side, x)):
        pl.semaphore_signal(barrier, inc=1, device_id=d, device_id_type=MESH)
    pl.semaphore_wait(barrier, 10)

    def send(src, dst, s_sem, r_sem, where):
        cp = pltpu.make_async_remote_copy(src_ref=src, dst_ref=dst, send_sem=s_sem, recv_sem=r_sem,
                                          device_id=where, device_id_type=MESH)
        cp.start()

    def arrived(ref, sem):
        pltpu.make_async_copy(ref, ref, sem).wait()

    in_plane = plane_of(z, y) == x

    def final_ref(t, kind, zs, ys, xs):
        return b_all.at[t, lax.rem(ys, 2), zs // 2, kind, :, pl.ds(pl.multiple_of(xs * HALF, HALF), HALF)]

    def move_copies(t, kind):
        s, h = t // 2, t % 2
        src = b_hbm.at[pl.ds(s * BLOCK + kind * HALF, HALF), pl.ds(h * HALF, HALF)]
        off_z, off_y = offsets(kind, h, x)
        zt, yt = moved(kind, False, z, y, off_z, off_y)
        stay = x == (3 if h else 0)
        for direct in (True, False):
            dst = final_ref(t, kind, z, y, x) if direct else staged.at[t, kind]
            sem = b_recv.at[t, 0] if direct else m_recv.at[t, kind]
            cond = in_plane if direct else jnp.logical_not(in_plane)
            yield (jnp.logical_and(cond, stay), pltpu.make_async_copy(src, dst, sem), False)
            yield (jnp.logical_and(cond, jnp.logical_not(stay)),
                   pltpu.make_async_remote_copy(src_ref=src, dst_ref=dst, send_sem=sent.at[1], recv_sem=sem,
                                                device_id=dev(zt, yt, x), device_id_type=MESH), True)

    def move(t):
        for kind in range(2):
            for cond, cp, _ in move_copies(t, kind):
                pl.when(cond)(cp.start)

    def enter_copy(t, kind):
        off_z, off_y = offsets(kind, t % 2, x)
        zs, ys = moved(kind, True, z, y, off_z, off_y)
        xt = plane_of(zs, ys)
        cp = pltpu.make_async_remote_copy(src_ref=staged.at[t, kind], dst_ref=final_ref(t, kind, zs, ys, x),
                                          send_sem=sent.at[2], recv_sem=b_recv.at[t, 0],
                                          device_id=dev(z, y, xt), device_id_type=MESH)
        return xt != x, cp

    def enter(t):
        for kind in range(2):
            cond, cp = enter_copy(t, kind)

            @pl.when(cond)
            def _():
                arrived(staged.at[t, kind], m_recv.at[t, kind])
                cp.start()

    for t in range(MOVE_FIRST):
        move(t)

    for s in range(SLABS):
        src, dst = slab_copy(s)
        send(src, dst, sent.at[0], l_recv.at[s], partner)

    def unit_ref(t, kind, zt, yt):
        off_z, blk, par, off_y = root_info(kind, zt, yt)
        v = 2 * off_z + off_y if kind == 0 else 2 * off_y + off_z
        xs = 3 - v if t % 2 else v
        return b_all.at[t, par, blk, kind, :, pl.ds(pl.multiple_of(xs * HALF, HALF), HALF)]

    def region_ref(t, kind, zt, yt, half):
        off_z, blk, par, off_y = root_info(kind, zt, yt)
        pair = off_z if kind == 0 else off_y
        cols = pl.ds(pl.multiple_of((1 - pair if t % 2 else pair) * 256, 256), 256)
        if kind == 0:
            return b_all.at[t, half, blk, 0, :, cols]
        return b_all.at[t, par, half, 1, :, cols]

    lo_pos = [(z, _rem4(y - 1)), (_rem4(z - 1), y)]
    hi_pos = [(z, _rem4(y + 1)), (_rem4(z + 1), y)]
    lo_dev, hi_dev = [y_lo, z_lo], [y_hi, z_hi]
    any_unit = b_all.at[0, 0, 0, 0, :, pl.ds(0, HALF)]
    any_region = b_all.at[0, 0, 0, 0, :, pl.ds(0, 256)]

    def unit_own(t, kind):
        ref, up = unit_ref(t, kind, z, y), (t + kind) % 2 == 0
        send(ref, ref, sent.at[3], b_recv.at[t, 1 if up else 2], hi_dev[kind])
        send(ref, ref, sent.at[3], b_recv.at[t, 2 if up else 1], lo_dev[kind])

    def unit_relay(t, kind):
        up = (t + kind) % 2 == 0
        ref = unit_ref(t, kind, *(lo_pos if up else hi_pos)[kind])
        send(ref, ref, sent.at[3], b_recv.at[t, 2], (hi_dev if up else lo_dev)[kind])

    def region_own(t, kind):
        axis = 1 - kind
        for j in range(2):
            up, down = region_ref(t, kind, z, y, j), region_ref(t, kind, z, y, 1 - j)
            send(up, up, sent.at[4], b_recv.at[t, 7 if j else 3 + 2 * kind], hi_dev[axis])
            send(down, down, sent.at[4], b_recv.at[t, 7 if j else 4 + 2 * kind], lo_dev[axis])

    def region_relay(t, kind):
        axis = 1 - kind
        arrived(any_region, b_recv.at[t, 3 + 2 * kind])
        ref = region_ref(t, kind, *lo_pos[axis], 0)
        send(ref, ref, sent.at[4], b_recv.at[t, 7], hi_dev[axis])
        arrived(any_region, b_recv.at[t, 4 + 2 * kind])
        ref = region_ref(t, kind, *hi_pos[axis], 1)
        send(ref, ref, sent.at[4], b_recv.at[t, 7], lo_dev[axis])

    def first_own(t):
        arrived(staged.at[t], b_recv.at[t, 0])
        for kind in range(2):
            unit_own(t, kind)

    def first_relay(t):
        arrived(staged.at[t], b_recv.at[t, 1])
        for kind in range(2):
            unit_relay(t, kind)

    def second_own(t):
        arrived(staged.at[0:2], b_recv.at[t, 2])
        for kind in range(2):
            region_own(t, kind)

    def second_relay(t):
        for kind in range(2):
            region_relay(t, kind)

    def product(t, sp):
        s, h = t // 2, t % 2
        lhs = l_all[s, sp * BLOCK:(sp + 1) * BLOCK, :]
        for n in range(2):
            rhs = b_all[t, :, :, :, :, n * 256:(n + 1) * 256].reshape(1024, 256)
            p = jnp.dot(lhs, rhs, preferred_element_type=F32)
            for j in range(2):
                part = p[:, j * HALF:(j + 1) * HALF]
                if s > 0:
                    part = part + acc[sp, h, 2 * n + j]
                acc[sp, h, 2 * n + j] = part

    def compute(t):
        s = t // 2
        arrived(b_all.at[t, 0], b_recv.at[t, 7])
        if t % 2 == 0:
            arrived(l_all.at[s, pl.ds(s * BLOCK, 1024 - s * BLOCK), :], l_recv.at[s])
        product(t, s)

    def part_ref(t, slot, half):
        return acc.at[t // 2, t % 2, slot, pl.ds(half * HALF, HALF), :]

    xp1, xm1, xp2 = _rem4(x + 1), _rem4(x - 1), _rem4(x + 2)

    def reduce_first(t):
        send(part_ref(t, xp2, 0), relay_lo.at[t], sent.at[5], r_recv.at[t, 0], x_hi)
        send(part_ref(t, xp2, 1), relay_hi.at[t], sent.at[5], r_recv.at[t, 1], x_lo)
        send(part_ref(t, xp1, 1), from_lo.at[t, pl.ds(HALF, HALF), :], sent.at[5], r_recv.at[t, 2], x_hi)
        send(part_ref(t, xm1, 0), from_hi.at[t, pl.ds(0, HALF), :], sent.at[5], r_recv.at[t, 2], x_lo)

    def reduce_second(t):
        s, h = t // 2, t % 2
        arrived(relay_lo.at[t], r_recv.at[t, 0])
        acc[s, h, xp1, 0:HALF, :] = acc[s, h, xp1, 0:HALF, :] + relay_lo[t]
        send(part_ref(t, xp1, 0), from_lo.at[t, pl.ds(0, HALF), :], sent.at[5], r_recv.at[t, 2], x_hi)
        arrived(relay_hi.at[t], r_recv.at[t, 1])
        acc[s, h, xm1, HALF:BLOCK, :] = acc[s, h, xm1, HALF:BLOCK, :] + relay_hi[t]
        send(part_ref(t, xm1, 1), from_hi.at[t, pl.ds(HALF, HALF), :], sent.at[5], r_recv.at[t, 2], x_lo)

    def finish(t):
        s, h = t // 2, t % 2
        arrived(from_lo.at[0:2], r_recv.at[t, 2])
        total = acc[s, h, x] + from_lo[t] + from_hi[t]
        out_ref[s * BLOCK:(s + 1) * BLOCK, h * HALF:(h + 1) * HALF] = total.astype(out_ref.dtype)

    def others(t):
        for sp in range(t // 2 + 1, SLABS):
            product(t, sp)

    steps = {"move": move, "enter": enter, "own1": first_own, "relay1": first_relay, "own2": second_own, "relay2": second_relay,
             "compute": compute, "reduce1": reduce_first, "others": others, "reduce2": reduce_second, "finish": finish}
    for i in range(-4, STAGES + 8):
        for name, lag in ORDER:
            t = i - lag
            if 0 <= t < STAGES and not (name == "move" and t < MOVE_FIRST):
                steps[name](t)

    arrived(l_all.at[:, 0:320, :], sent.at[0])
    for i, few in ((1, jnp.logical_or(x == 0, x == 3)), (2, jnp.logical_or(plane_of(z, y) == 0, plane_of(z, y) == 3))):
        @pl.when(few)
        def _():
            arrived(staged.at[0:4], sent.at[i])

        @pl.when(jnp.logical_not(few))
        def _():
            arrived(staged, sent.at[i])
    arrived(l_all.at[0, 0:768, :], sent.at[3])
    arrived(b_all.at[0:6], sent.at[4])
    arrived(l_all.at[0:3, 0:512, :], sent.at[5])


def solution(mesh):
    def local_product(lower_loc, rhs_loc):
        rows, cols = rhs_loc.shape
        bf16 = lower_loc.dtype
        return pl.pallas_call(
            _kernel,
            out_shape=jax.ShapeDtypeStruct((rows, cols), bf16),
            in_specs=[pl.BlockSpec(memory_space=pltpu.HBM)] * 2,
            out_specs=pl.BlockSpec(memory_space=pltpu.VMEM),
            scratch_shapes=[
                pltpu.VMEM((SLABS, 1024, 1024), bf16),
                pltpu.VMEM((STAGES, 2, 2, 2, HALF, 512), bf16),
                pltpu.VMEM((SLABS, 2, 4, BLOCK, HALF), F32),
                pltpu.VMEM((STAGES, HALF, HALF), F32),
                pltpu.VMEM((STAGES, HALF, HALF), F32),
                pltpu.VMEM((STAGES, BLOCK, HALF), F32),
                pltpu.VMEM((STAGES, BLOCK, HALF), F32),
                pltpu.VMEM((STAGES, 2, HALF, HALF), bf16),
                pltpu.SemaphoreType.DMA((SLABS,)),
                pltpu.SemaphoreType.DMA((STAGES, 2)),
                pltpu.SemaphoreType.DMA((STAGES, 8)),
                pltpu.SemaphoreType.DMA((STAGES, 3)),
                pltpu.SemaphoreType.DMA((6,)),
            ],
            compiler_params=pltpu.CompilerParams(collective_id=0, has_side_effects=True, vmem_limit_bytes=63 * 1024 * 1024),
        )(lower_loc, rhs_loc)

    return jax.shard_map(local_product, mesh=mesh, in_specs=(P("row", "col"), P("row", ("batch", "col"))), out_specs=P("row", ("batch", "col")), check_vma=False)
```

time: 83 us -> 77 us (0.928)
  Pallas kernels: 80.9 us -> 74.9 us
    pallas_call x1, Pallas kernels: 80.9 us -> 74.9 us  [local_product(): pl.pallas_call(_kernel, out_shape=jax.ShapeDtypeStruct((rows, cols), bf16...]
where the time goes in v3:
time: 77 us; the launch traced here: 76.7 us
  Pallas kernels  74.9 us (97%)
  local copies, waits for them, and re-layouts  1.87 us (2%)
    pallas_call x1, Pallas kernels, local_product(): pl.pallas_call(_kernel, out_shape=jax.ShapeDtypeStruct((rows, cols), bf16...  74.9 us
    unnamed x1, local copies, waits for them, and re-layouts  1.87 us

profile of v3, /device:TPU:0, one launch (start us, length us, event | category | flops | bytes accessed | tf_op | source)
XLA Modules:
  0.0 76.7 jit_solution(8399044343101068289)
XLA Ops:
  0.0 74.9 %shard_map.28 = bf16[1024,256]{1,0:T(8,128)(2,1)} custom-call(bf16[1024,2048]{1,0:T(8,128)(2,1)} %l_hbm.1, bf16[1024,256]{1,0:T(8,128)(2,1)} %b_hbm.1), custom_call_target="tpu_custom_call" | custom-call | tf_op jit(solution)/shard_map/pallas_call | solution.py:271
  74.9 1.9 %copy.4 = bf16[1024,256]{1,0:T(8,128)(2,1)} copy(bf16[1024,256]{1,0:T(8,128)(2,1)} %shard_map.28) | data formatting | bytes 1048576

commit v4 on v3

--- a/solution.py
+++ b/solution.py
@@ -11,9 +11,26 @@
 SLABS = 4
 MESH = pl.DeviceIdType.MESH
 F32 = jnp.float32
-MOVE_FIRST = 8
-ORDER = (("move", -2), ("enter", -1), ("own1", 0), ("relay1", 1), ("own2", 2), ("relay2", 3), ("compute", 4), ("reduce1", 4),
-         ("reduce2", 5), ("others", 4), ("finish", 7))
+MASKS = (0, 3, 1, 2, 0, 3, 1, 2)
+AHEAD = (3, 4, 2)
+DIRECT = 1
+ROUND = (("relay2", 0), ("own2", 2), ("compute", -1), ("reduce1", -1), ("reduce2", -2), ("others", -1), ("finish", -4))
+
+
+def _program_order():
+    first, names = [], ("enter", "own1", "relay1")
+    for i in range(5 * STAGES):
+        lag = 0
+        for k, name in enumerate(names):
+            if 0 <= i - lag < STAGES:
+                first.append((name, i - lag))
+            lag += AHEAD[k]
+        for t in range(2):
+            if i == lag + t:
+                first.append(("own2", t))
+    second = [(name, i + d) for i in range(-2, STAGES + 6) for name, d in ROUND
+              if 0 <= i + d < STAGES and not (name == "own2" and i + d < 2)]
+    return first + second
 
 
 def _rem4(v):
@@ -21,7 +38,7 @@
 
 
 def _kernel(l_hbm, b_hbm, out_ref, l_all, b_all, acc, relay_lo, relay_hi, from_lo, from_hi,
-            staged, l_recv, m_recv, b_recv, r_recv, sent):
+            staged, b_home, l_recv, m_recv, b_recv, r_recv, sent, home_sem, out_buf):
     row = lax.axis_index("row")
     col = lax.axis_index("col")
     z, y = row // 4, lax.rem(row, 4)
@@ -35,8 +52,13 @@
     x_lo, x_hi = dev(z, y, _rem4(x - 1)), dev(z, y, _rem4(x + 1))
     partner = dev(z, y, x, 1 - core)
 
-    def offsets(kind, h, xs):
-        v = 3 - xs if h else xs
+    def mix(t, v):
+        m = MASKS[t]
+        v = v if m % 2 == 0 else v + 1 - 2 * lax.rem(v, 2)
+        return v if m < 2 else lax.rem(v + 2, 4)
+
+    def offsets(kind, t, xs):
+        v = mix(t, xs)
         hi, lo = v // 2, lax.rem(v, 2)
         return (hi, lo) if kind == 0 else (lo, hi)
 
@@ -59,16 +81,20 @@
         rows = pl.ds(s * BLOCK, 1024 - s * BLOCK)
         return l_hbm.at[rows, pl.ds(s * 512, 512)], l_all.at[s, rows, pl.ds(pl.multiple_of(core * 512, 512), 512)]
 
+    home_copy = pltpu.make_async_copy(b_hbm, b_home, home_sem)
+    home_copy.start()
     for s in range(SLABS):
         src, dst = slab_copy(s)
         pltpu.make_async_copy(src, dst, l_recv.at[s]).start()
 
     barrier = pltpu.get_barrier_semaphore()
+    y_far, z_far = dev(z, _rem4(y + 2), x), dev(_rem4(z + 2), y, x)
     y_side = _rem4(y + 2 * lax.rem(y, 2) - 1)
-    for d in (z_lo, z_hi, y_lo, y_hi, x_lo, x_hi, dev(z, y, _rem4(x + 2)), partner,
+    for d in (z_lo, z_hi, y_lo, y_hi, x_lo, x_hi, dev(z, y, _rem4(x + 2)), partner, y_far, z_far,
               dev(_rem4(z - 1), y_side, x), dev(_rem4(z + 1), y_side, x)):
         pl.semaphore_signal(barrier, inc=1, device_id=d, device_id_type=MESH)
-    pl.semaphore_wait(barrier, 10)
+    home_copy.wait()
+    pl.semaphore_wait(barrier, 12)
 
     def send(src, dst, s_sem, r_sem, where):
         cp = pltpu.make_async_remote_copy(src_ref=src, dst_ref=dst, send_sem=s_sem, recv_sem=r_sem,
@@ -85,17 +111,17 @@
 
     def move_copies(t, kind):
         s, h = t // 2, t % 2
-        src = b_hbm.at[pl.ds(s * BLOCK + kind * HALF, HALF), pl.ds(h * HALF, HALF)]
-        off_z, off_y = offsets(kind, h, x)
+        here = (pl.ds(s * BLOCK + kind * HALF, HALF), pl.ds(h * HALF, HALF))
+        off_z, off_y = offsets(kind, t, x)
         zt, yt = moved(kind, False, z, y, off_z, off_y)
-        stay = x == (3 if h else 0)
+        stay = x == MASKS[t]
         for direct in (True, False):
             dst = final_ref(t, kind, z, y, x) if direct else staged.at[t, kind]
             sem = b_recv.at[t, 0] if direct else m_recv.at[t, kind]
             cond = in_plane if direct else jnp.logical_not(in_plane)
-            yield (jnp.logical_and(cond, stay), pltpu.make_async_copy(src, dst, sem), False)
+            yield (jnp.logical_and(cond, stay), pltpu.make_async_copy(b_hbm.at[here], dst, sem), False)
             yield (jnp.logical_and(cond, jnp.logical_not(stay)),
-                   pltpu.make_async_remote_copy(src_ref=src, dst_ref=dst, send_sem=sent.at[1], recv_sem=sem,
+                   pltpu.make_async_remote_copy(src_ref=b_home.at[here], dst_ref=dst, send_sem=sent.at[1], recv_sem=sem,
                                                 device_id=dev(zt, yt, x), device_id_type=MESH), True)
 
     def move(t):
@@ -104,7 +130,7 @@
                 pl.when(cond)(cp.start)
 
     def enter_copy(t, kind):
-        off_z, off_y = offsets(kind, t % 2, x)
+        off_z, off_y = offsets(kind, t, x)
         zs, ys = moved(kind, True, z, y, off_z, off_y)
         xt = plane_of(zs, ys)
         cp = pltpu.make_async_remote_copy(src_ref=staged.at[t, kind], dst_ref=final_ref(t, kind, zs, ys, x),
@@ -121,7 +147,7 @@
                 arrived(staged.at[t, kind], m_recv.at[t, kind])
                 cp.start()
 
-    for t in range(MOVE_FIRST):
+    for t in range(STAGES):
         move(t)
 
     for s in range(SLABS):
@@ -131,25 +157,29 @@
     def unit_ref(t, kind, zt, yt):
         off_z, blk, par, off_y = root_info(kind, zt, yt)
         v = 2 * off_z + off_y if kind == 0 else 2 * off_y + off_z
-        xs = 3 - v if t % 2 else v
+        xs = mix(t, v)
         return b_all.at[t, par, blk, kind, :, pl.ds(pl.multiple_of(xs * HALF, HALF), HALF)]
 
     def region_ref(t, kind, zt, yt, half):
         off_z, blk, par, off_y = root_info(kind, zt, yt)
         pair = off_z if kind == 0 else off_y
-        cols = pl.ds(pl.multiple_of((1 - pair if t % 2 else pair) * 256, 256), 256)
+        cols = pl.ds(pl.multiple_of((pair if MASKS[t] < 2 else 1 - pair) * 256, 256), 256)
         if kind == 0:
             return b_all.at[t, half, blk, 0, :, cols]
         return b_all.at[t, par, half, 1, :, cols]
 
     lo_pos = [(z, _rem4(y - 1)), (_rem4(z - 1), y)]
     hi_pos = [(z, _rem4(y + 1)), (_rem4(z + 1), y)]
-    lo_dev, hi_dev = [y_lo, z_lo], [y_hi, z_hi]
+    lo_dev, hi_dev, far_dev = [y_lo, z_lo], [y_hi, z_hi], [y_far, z_far]
     any_unit = b_all.at[0, 0, 0, 0, :, pl.ds(0, HALF)]
     any_region = b_all.at[0, 0, 0, 0, :, pl.ds(0, 256)]
 
     def unit_own(t, kind):
         ref, up = unit_ref(t, kind, z, y), (t + kind) % 2 == 0
+        if t < DIRECT:
+            for d in (hi_dev[kind], lo_dev[kind], far_dev[kind]):
+                send(ref, ref, sent.at[3], b_recv.at[t, 2], d)
+            return
         send(ref, ref, sent.at[3], b_recv.at[t, 1 if up else 2], hi_dev[kind])
         send(ref, ref, sent.at[3], b_recv.at[t, 2 if up else 1], lo_dev[kind])
 
@@ -180,12 +210,14 @@
             unit_own(t, kind)
 
     def first_relay(t):
+        if t < DIRECT:
+            return
         arrived(staged.at[t], b_recv.at[t, 1])
         for kind in range(2):
             unit_relay(t, kind)
 
     def second_own(t):
-        arrived(staged.at[0:2], b_recv.at[t, 2])
+        arrived(staged.at[0:3] if t < DIRECT else staged.at[0:2], b_recv.at[t, 2])
         for kind in range(2):
             region_own(t, kind)
 
@@ -236,32 +268,25 @@
         s, h = t // 2, t % 2
         arrived(from_lo.at[0:2], r_recv.at[t, 2])
         total = acc[s, h, x] + from_lo[t] + from_hi[t]
-        out_ref[s * BLOCK:(s + 1) * BLOCK, h * HALF:(h + 1) * HALF] = total.astype(out_ref.dtype)
+        out_buf[t] = total.astype(out_buf.dtype)
+        pltpu.make_async_copy(out_buf.at[t], out_ref.at[pl.ds(s * BLOCK, BLOCK), pl.ds(h * HALF, HALF)], home_sem).start()
 
     def others(t):
         for sp in range(t // 2 + 1, SLABS):
             product(t, sp)
 
-    steps = {"move": move, "enter": enter, "own1": first_own, "relay1": first_relay, "own2": second_own, "relay2": second_relay,
+    steps = {"enter": enter, "own1": first_own, "relay1": first_relay, "own2": second_own, "relay2": second_relay,
              "compute": compute, "reduce1": reduce_first, "others": others, "reduce2": reduce_second, "finish": finish}
-    for i in range(-4, STAGES + 8):
-        for name, lag in ORDER:
-            t = i - lag
-            if 0 <= t < STAGES and not (name == "move" and t < MOVE_FIRST):
-                steps[name](t)
+    for name, t in _program_order():
+        steps[name](t)
 
     arrived(l_all.at[:, 0:320, :], sent.at[0])
-    for i, few in ((1, jnp.logical_or(x == 0, x == 3)), (2, jnp.logical_or(plane_of(z, y) == 0, plane_of(z, y) == 3))):
-        @pl.when(few)
-        def _():
-            arrived(staged.at[0:4], sent.at[i])
-
-        @pl.when(jnp.logical_not(few))
-        def _():
-            arrived(staged, sent.at[i])
+    arrived(staged.at[0:6], sent.at[1])
+    arrived(staged.at[0:6], sent.at[2])
     arrived(l_all.at[0, 0:768, :], sent.at[3])
     arrived(b_all.at[0:6], sent.at[4])
     arrived(l_all.at[0:3, 0:512, :], sent.at[5])
+    arrived(out_buf, home_sem)
 
 
 def solution(mesh):
@@ -272,7 +297,7 @@
             _kernel,
             out_shape=jax.ShapeDtypeStruct((rows, cols), bf16),
             in_specs=[pl.BlockSpec(memory_space=pltpu.HBM)] * 2,
-            out_specs=pl.BlockSpec(memory_space=pltpu.VMEM),
+            out_specs=pl.BlockSpec(memory_space=pltpu.HBM),
             scratch_shapes=[
                 pltpu.VMEM((SLABS, 1024, 1024), bf16),
                 pltpu.VMEM((STAGES, 2, 2, 2, HALF, 512), bf16),
@@ -282,11 +307,14 @@
                 pltpu.VMEM((STAGES, BLOCK, HALF), F32),
                 pltpu.VMEM((STAGES, BLOCK, HALF), F32),
                 pltpu.VMEM((STAGES, 2, HALF, HALF), bf16),
+                pltpu.VMEM((rows, cols), bf16),
                 pltpu.SemaphoreType.DMA((SLABS,)),
                 pltpu.SemaphoreType.DMA((STAGES, 2)),
                 pltpu.SemaphoreType.DMA((STAGES, 8)),
                 pltpu.SemaphoreType.DMA((STAGES, 3)),
                 pltpu.SemaphoreType.DMA((6,)),
+                pltpu.SemaphoreType.DMA,
+                pltpu.VMEM((STAGES, BLOCK, HALF), bf16),
             ],
             compiler_params=pltpu.CompilerParams(collective_id=0, has_side_effects=True, vmem_limit_bytes=63 * 1024 * 1024),
         )(lower_loc, rhs_loc)

time: 77 us -> 75.3 us (0.978)
  Pallas kernels: 74.9 us -> 73.3 us
    pallas_call x1, Pallas kernels: 74.9 us -> 73.3 us  [local_product(): pl.pallas_call(_kernel, out_shape=jax.ShapeDtypeStruct((rows, cols), bf16...]
where the time goes in v4:
time: 75.3 us; the launch traced here: 75.2 us
  Pallas kernels  73.3 us (97%)
  local copies, waits for them, and re-layouts  1.87 us (2%)
    pallas_call x1, Pallas kernels, local_product(): pl.pallas_call(_kernel, out_shape=jax.ShapeDtypeStruct((rows, cols), bf16...  73.3 us
    unnamed x1, local copies, waits for them, and re-layouts  1.87 us

profile of v4, /device:TPU:0, one launch (start us, length us, event | category | flops | bytes accessed | tf_op | source)
XLA Modules:
  0.0 75.2 jit_solution(2384545791323322534)
XLA Ops:
  0.0 73.3 %shard_map.28 = bf16[1024,256]{1,0:T(8,128)(2,1)} custom-call(bf16[1024,2048]{1,0:T(8,128)(2,1)} %l_hbm.1, bf16[1024,256]{1,0:T(8,128)(2,1)} %b_hbm.1), custom_call_target="tpu_custom_call" | custom-call | tf_op jit(solution)/shard_map/pallas_call | solution.py:296
  73.3 1.9 %copy.4 = bf16[1024,256]{1,0:T(8,128)(2,1)} copy(bf16[1024,256]{1,0:T(8,128)(2,1)} %shard_map.28) | data formatting | bytes 1048576

commit v5 on v4

--- a/solution.py
+++ b/solution.py
@@ -11,9 +11,10 @@
 SLABS = 4
 MESH = pl.DeviceIdType.MESH
 F32 = jnp.float32
-MASKS = (0, 3, 1, 2, 0, 3, 1, 2)
+MASKS = (2, 1, 0, 3, 2, 1, 0, 3)
 AHEAD = (3, 4, 2)
-DIRECT = 1
+DIRECT = 2
+FINE, PIECES = 1, 2
 ROUND = (("relay2", 0), ("own2", 2), ("compute", -1), ("reduce1", -1), ("reduce2", -2), ("others", -1), ("finish", -4))
 
 
@@ -38,7 +39,7 @@
 
 
 def _kernel(l_hbm, b_hbm, out_ref, l_all, b_all, acc, relay_lo, relay_hi, from_lo, from_hi,
-            staged, b_home, l_recv, m_recv, b_recv, r_recv, sent, home_sem, out_buf):
+            staged, b_home, l_recv, m_recv, b_recv, r_recv, sent, home_sem, out_buf, fine_recv):
     row = lax.axis_index("row")
     col = lax.axis_index("col")
     z, y = row // 4, lax.rem(row, 4)
@@ -225,12 +226,14 @@
         for kind in range(2):
             region_relay(t, kind)
 
-    def product(t, sp):
+    xp1, xm1, xp2 = _rem4(x + 1), _rem4(x - 1), _rem4(x + 2)
+
+    def product(t, sp, halves):
         s, h = t // 2, t % 2
         lhs = l_all[s, sp * BLOCK:(sp + 1) * BLOCK, :]
-        for n in range(2):
-            rhs = b_all[t, :, :, :, :, n * 256:(n + 1) * 256].reshape(1024, 256)
-            p = jnp.dot(lhs, rhs, preferred_element_type=F32)
+        for n in halves:
+            cols = pl.ds(n * 256 if isinstance(n, int) else pl.multiple_of(n * 256, 256), 256)
+            p = jnp.dot(lhs, b_all[t, :, :, :, :, cols].reshape(1024, 256), preferred_element_type=F32)
             for j in range(2):
                 part = p[:, j * HALF:(j + 1) * HALF]
                 if s > 0:
@@ -242,27 +245,35 @@
         arrived(b_all.at[t, 0], b_recv.at[t, 7])
         if t % 2 == 0:
             arrived(l_all.at[s, pl.ds(s * BLOCK, 1024 - s * BLOCK), :], l_recv.at[s])
-        product(t, s)
+        product(t, s, [xp2 // 2])
 
     def part_ref(t, slot, half):
         return acc.at[t // 2, t % 2, slot, pl.ds(half * HALF, HALF), :]
 
-    xp1, xm1, xp2 = _rem4(x + 1), _rem4(x - 1), _rem4(x + 2)
+    def pieces(t):
+        n = PIECES if t >= STAGES - FINE else 1
+        rows = HALF // n
+        for q in range(n):
+            sems = [fine_recv.at[t - STAGES + FINE, k, q] if n > 1 else r_recv.at[t, k] for k in range(2)]
+            yield q * rows, rows, sems
 
     def reduce_first(t):
-        send(part_ref(t, xp2, 0), relay_lo.at[t], sent.at[5], r_recv.at[t, 0], x_hi)
-        send(part_ref(t, xp2, 1), relay_hi.at[t], sent.at[5], r_recv.at[t, 1], x_lo)
+        s, h = t // 2, t % 2
+        for r0, rows, sems in pieces(t):
+            send(acc.at[s, h, xp2, pl.ds(r0, rows), :], relay_lo.at[t, pl.ds(r0, rows), :], sent.at[5], sems[0], x_hi)
+            send(acc.at[s, h, xp2, pl.ds(HALF + r0, rows), :], relay_hi.at[t, pl.ds(r0, rows), :], sent.at[5], sems[1], x_lo)
+        product(t, s, [1 - xp2 // 2])
         send(part_ref(t, xp1, 1), from_lo.at[t, pl.ds(HALF, HALF), :], sent.at[5], r_recv.at[t, 2], x_hi)
         send(part_ref(t, xm1, 0), from_hi.at[t, pl.ds(0, HALF), :], sent.at[5], r_recv.at[t, 2], x_lo)
 
     def reduce_second(t):
         s, h = t // 2, t % 2
-        arrived(relay_lo.at[t], r_recv.at[t, 0])
-        acc[s, h, xp1, 0:HALF, :] = acc[s, h, xp1, 0:HALF, :] + relay_lo[t]
-        send(part_ref(t, xp1, 0), from_lo.at[t, pl.ds(0, HALF), :], sent.at[5], r_recv.at[t, 2], x_hi)
-        arrived(relay_hi.at[t], r_recv.at[t, 1])
-        acc[s, h, xm1, HALF:BLOCK, :] = acc[s, h, xm1, HALF:BLOCK, :] + relay_hi[t]
-        send(part_ref(t, xm1, 1), from_hi.at[t, pl.ds(HALF, HALF), :], sent.at[5], r_recv.at[t, 2], x_lo)
+        for r0, rows, sems in pieces(t):
+            for sem, relay, slot, base, dst, to in ((sems[0], relay_lo, xp1, 0, from_lo, x_hi), (sems[1], relay_hi, xm1, HALF, from_hi, x_lo)):
+                here = pl.ds(base + r0, rows)
+                arrived(relay.at[t, pl.ds(r0, rows), :], sem)
+                acc[s, h, slot, here, :] = acc[s, h, slot, here, :] + relay[t, pl.ds(r0, rows), :]
+                send(acc.at[s, h, slot, here, :], dst.at[t, here, :], sent.at[5], r_recv.at[t, 2], to)
 
     def finish(t):
         s, h = t // 2, t % 2
@@ -273,7 +284,7 @@
 
     def others(t):
         for sp in range(t // 2 + 1, SLABS):
-            product(t, sp)
+            product(t, sp, range(2))
 
     steps = {"enter": enter, "own1": first_own, "relay1": first_relay, "own2": second_own, "relay2": second_relay,
              "compute": compute, "reduce1": reduce_first, "others": others, "reduce2": reduce_second, "finish": finish}
@@ -315,6 +326,7 @@
                 pltpu.SemaphoreType.DMA((6,)),
                 pltpu.SemaphoreType.DMA,
                 pltpu.VMEM((STAGES, BLOCK, HALF), bf16),
+                pltpu.SemaphoreType.DMA((FINE, 2, PIECES)),
             ],
             compiler_params=pltpu.CompilerParams(collective_id=0, has_side_effects=True, vmem_limit_bytes=63 * 1024 * 1024),
         )(lower_loc, rhs_loc)

time: 75.3 us -> 74.7 us (level)
  no operation moved by 1% of the time
where the time goes in v5:
time: 74.7 us; the launch traced here: 74.6 us
  Pallas kernels  72.7 us (97%)
  local copies, waits for them, and re-layouts  1.87 us (3%)
    pallas_call x1, Pallas kernels, local_product(): pl.pallas_call(_kernel, out_shape=jax.ShapeDtypeStruct((rows, cols), bf16...  72.7 us
    unnamed x1, local copies, waits for them, and re-layouts  1.87 us

profile of v5, /device:TPU:0, one launch (start us, length us, event | category | flops | bytes accessed | tf_op | source)
XLA Modules:
  0.0 74.6 jit_solution(2756933366067783599)
XLA Ops:
  0.0 72.7 %shard_map.28 = bf16[1024,256]{1,0:T(8,128)(2,1)} custom-call(bf16[1024,2048]{1,0:T(8,128)(2,1)} %l_hbm.1, bf16[1024,256]{1,0:T(8,128)(2,1)} %b_hbm.1), custom_call_target="tpu_custom_call" | custom-call | tf_op jit(solution)/shard_map/pallas_call | solution.py:307
  72.7 1.9 %copy.4 = bf16[1024,256]{1,0:T(8,128)(2,1)} copy(bf16[1024,256]{1,0:T(8,128)(2,1)} %shard_map.28) | data formatting | bytes 1048576

commit v6 on v5

--- a/solution.py
+++ b/solution.py
@@ -11,7 +11,7 @@
 SLABS = 4
 MESH = pl.DeviceIdType.MESH
 F32 = jnp.float32
-MASKS = (2, 1, 0, 3, 2, 1, 0, 3)
+MASKS = (2, 1, 2, 1, 0, 3, 0, 3)
 AHEAD = (3, 4, 2)
 DIRECT = 2
 FINE, PIECES = 1, 2

time: 74.7 us -> 74.5 us (level)
  no operation moved by 1% of the time
where the time goes in v6:
time: 74.5 us; the launch traced here: 74.4 us
  Pallas kernels  72.5 us (97%)
  local copies, waits for them, and re-layouts  1.87 us (3%)
    pallas_call x1, Pallas kernels, local_product(): pl.pallas_call(_kernel, out_shape=jax.ShapeDtypeStruct((rows, cols), bf16...  72.5 us
    unnamed x1, local copies, waits for them, and re-layouts  1.87 us

profile of v6, /device:TPU:0, one launch (start us, length us, event | category | flops | bytes accessed | tf_op | source)
XLA Modules:
  0.0 74.4 jit_solution(1269485959388327654)
XLA Ops:
  0.0 72.5 %shard_map.28 = bf16[1024,256]{1,0:T(8,128)(2,1)} custom-call(bf16[1024,2048]{1,0:T(8,128)(2,1)} %l_hbm.1, bf16[1024,256]{1,0:T(8,128)(2,1)} %b_hbm.1), custom_call_target="tpu_custom_call" | custom-call | tf_op jit(solution)/shard_map/pallas_call | solution.py:307
  72.5 1.9 %copy.4 = bf16[1024,256]{1,0:T(8,128)(2,1)} copy(bf16[1024,256]{1,0:T(8,128)(2,1)} %shard_map.28) | data formatting | bytes 1048576

commit v7 on v6

--- a/solution.py
+++ b/solution.py
@@ -11,7 +11,7 @@
 SLABS = 4
 MESH = pl.DeviceIdType.MESH
 F32 = jnp.float32
-MASKS = (2, 1, 2, 1, 0, 3, 0, 3)
+MASKS = (2, 2, 1, 1, 0, 3, 0, 3)
 AHEAD = (3, 4, 2)
 DIRECT = 2
 FINE, PIECES = 1, 2

time: 74.5 us -> 74.4 us (level)
  no operation moved by 1% of the time
where the time goes in v7:
time: 74.4 us; the launch traced here: 74.2 us
  Pallas kernels  72.3 us (97%)
  local copies, waits for them, and re-layouts  1.87 us (3%)
    pallas_call x1, Pallas kernels, local_product(): pl.pallas_call(_kernel, out_shape=jax.ShapeDtypeStruct((rows, cols), bf16...  72.3 us
    unnamed x1, local copies, waits for them, and re-layouts  1.87 us

profile of v7, /device:TPU:0, one launch (start us, length us, event | category | flops | bytes accessed | tf_op | source)
XLA Modules:
  0.0 74.2 jit_solution(5106620892165272869)
XLA Ops:
  0.0 72.3 %shard_map.28 = bf16[1024,256]{1,0:T(8,128)(2,1)} custom-call(bf16[1024,2048]{1,0:T(8,128)(2,1)} %l_hbm.1, bf16[1024,256]{1,0:T(8,128)(2,1)} %b_hbm.1), custom_call_target="tpu_custom_call" | custom-call | tf_op jit(solution)/shard_map/pallas_call | solution.py:307
  72.3 1.9 %copy.4 = bf16[1024,256]{1,0:T(8,128)(2,1)} copy(bf16[1024,256]{1,0:T(8,128)(2,1)} %shard_map.28) | data formatting | bytes 1048576
